TPU v7x, 32 devices: a whole 2x2x4 slice. The times are simulated.
32 devices in a mesh: wide: 8 (over y, x, core), narrow: 4 (over z).
Axes of the slice: x: 2, y: 2, z: 4, core: 2. Of those that a mesh axis runs over, the one named last changes fastest.
Arguments:
- local_slopes: float32 [32, 512, 128], P(('wide', 'narrow')), may hold values from -0.25 to 0.25
- global_slopes: float32 [32, 512, 1024], P(('wide', 'narrow')), may hold values from -0.25 to 0.25
- residuals: float32 [32, 512], P(('wide', 'narrow')), may hold values from -6 to 6
- weights: float32 [32, 512], P(('wide', 'narrow')), may hold values from 0.1 to 10
- track_slot_count: int32 [32], P(('wide', 'narrow')), may hold values from 64 to 512
- windows: int32 [32], P(('wide', 'narrow')), may hold values from 0 to 3
Outputs:
- normal_matrix: float32 [4, 1024, 1024], P(None, 'narrow', 'wide')
- normal_rhs: float32 [4, 1024], P(None, 'narrow')
All inputs are finite; a program needn't handle non-finite values.
Results may differ from a plain program's by a relative error of at most 0.0003.
Values sent between devices are 32-bit elements; how exact they have to be, the bound alone decides.
A program may use at most 64 MiB of HBM per device.

v0:
```python
import jax
import jax.numpy as jnp
from jax import lax
from jax.sharding import PartitionSpec as P

WINDOW_PARAMS = 1024
NWIN = 4


def tdot(left, right):
    return lax.dot_general(
        left,
        right,
        (((0,), (0,)), ((), ())),
        precision=lax.Precision.HIGHEST,
        preferred_element_type=jnp.float32,
    )


def rows_product(left, right):
    return tdot(left, right)


def window_sum(window_ids, stacked):
    picks = (window_ids[:, None] == jnp.arange(NWIN, dtype=jnp.int32)[None, :]).astype(jnp.float32)
    return jnp.einsum(
        "bw,bij->wij",
        picks,
        stacked,
        precision=lax.Precision.HIGHEST,
        preferred_element_type=jnp.float32,
    )


def on_device(local_slopes, global_slopes, residuals, weights, track_slot_count, windows):
    bundle_count, measure_slot, local_param = local_slopes.shape
    slot_entries = jnp.arange(measure_slot, dtype=jnp.int32)
    count = track_slot_count[0]
    local_b = local_slopes[0]
    global_b = global_slopes[0]
    resid_b = residuals[0][:, None]
    live = jnp.where(slot_entries < count, weights[0], jnp.float32(0.0))
    wl = local_b * live[:, None]
    wg = global_b * live[:, None]
    curv = rows_product(wl, local_b) + jnp.eye(local_param, dtype=jnp.float32)
    lr = rows_product(wl, resid_b)
    gr = rows_product(wg, resid_b)[:, 0]
    coupling = rows_product(wl, global_b)
    gram = rows_product(wg, global_b)
    factor = jnp.linalg.cholesky(curv)
    solved = jax.scipy.linalg.cho_solve((factor, True), jnp.concatenate([coupling, lr], axis=1))
    schurs = [gram - tdot(coupling, solved[:, :WINDOW_PARAMS])]
    reduced = [gr - tdot(coupling, solved[:, WINDOW_PARAMS:])[:, 0]]
    stacked = jnp.stack(schurs, axis=0)
    rhs_stack = jnp.stack(reduced, axis=0)
    rhs_local = window_sum(windows, rhs_stack[:, :, None])[:, :, 0]
    rhs_whole = lax.psum(rhs_local, ("wide", "narrow"))
    owned = WINDOW_PARAMS // lax.axis_size("narrow")
    normal_rhs = lax.dynamic_slice_in_dim(rhs_whole, lax.axis_index("narrow") * owned, owned, 1)
    received = lax.all_to_all(stacked, "wide", split_axis=2, concat_axis=0, tiled=True)
    window_ids = lax.all_gather(windows, "wide", axis=0, tiled=True)
    partial_value = window_sum(window_ids, received)
    normal_matrix = lax.psum_scatter(partial_value, "narrow", scatter_dimension=1, tiled=True)
    return (normal_matrix, normal_rhs)


def solution(mesh):
    in_specs = (
        P(("wide", "narrow"), None, None),
        P(("wide", "narrow"), None, None),
        P(("wide", "narrow"), None),
        P(("wide", "narrow"), None),
        P(("wide", "narrow")),
        P(("wide", "narrow")),
    )
    out_specs = (P(None, "narrow", "wide"), P(None, "narrow"))
    return jax.shard_map(
        on_device, mesh=mesh, in_specs=in_specs, out_specs=out_specs, check_vma=False
    )
```

profile of v0, /device:TPU:0, one launch (start us, length us, event | category | flops | bytes accessed | tf_op | source)
XLA Modules:
  0.0 232.3 jit_solution(12225820016373866067)
XLA Ops:
  7.8 0.7 fusion.39
  8.5 1.7 fusion.18
  10.4 11.7 %cholesky.17 = f32[128,128]{1,0:T(8,128)S(1)} custom-call(f32[128,128]{1,0:T(8,128)S(1)} %fusion.34), custom_call_target="Cholesky" | custom-call | tf_op jit(solution)/shard_map/jit(cholesky)/cholesky | solution.py:50
  22.1 0.6 compare_reduce_fusion
  22.8 0.7 fusion.29
  23.4 9.8 %custom-call.10 = f32[1,128,128]{1,2,0:T(8,128)S(1)} custom-call(f32[1,128,128]{2,1,0:T(8,128)S(1)} %fusion.29), custom_call_target="InvertDiagBlocksLowerTriangular" | custom-call | tf_op jit(solution)/shard_map/jit(_cho_solve)/triangular_solve | solution.py:51
  33.3 1.6 convolution_bitcast_fusion
  34.9 3.1 %fusion.2 = f32[128,1024]{1,0:T(8,128)S(1)} fusion(f32[1,512,1024]{2,1,0:T(8,128)} %param.7, f32[1,512,128]{2,1,0:T(8,128)} %param.6, f32[512]{0:T(512)S(1)} %fusion.39), kind=kOutput, calls=%fused_computation.3 | convolution fusion | flops 805371904 | bytes 2885632 | tf_op jit(solution)/shard_map/dot_general | solution.py:11
  38.0 0.7 fusion.12
  38.7 1.1 fusion.30
  39.8 3.7 %fusion.16 = f32[1024,1024]{1,0:T(8,128)S(1)} fusion(f32[128,1024]{1,0:T(8,128)S(1)} %fusion.2, f32[128,1025]{0,1:T(8,128)S(1)} %fusion.30), kind=kOutput, calls=%fused_computation.18 | convolution fusion | flops 1610612736 | bytes 5242880 | tf_op jit(solution)/shard_map/dot_general | solution.py:11
  43.5 8.7 %subtract_bitcast_fusion = f32[1,1024,1024]{2,1,0:T(8,128)} fusion(f32[1024,1024]{1,0:T(8,128)S(1)} %fusion.16, f32[1,512,1024]{2,1,0:T(8,128)S(1)} %copy-done.1, f32[512]{0:T(512)S(1)} %fusion.39), kind=kOutput, calls=%fused_computation.2 | convolution fusion | flops 6444023808 | bytes 10487808 | tf_op jit(solution)/shard_map/dot_general | solution.py:11
  52.2 11.0 %copy.13 = f32[1,1024,1024]{1,0,2:T(1,128)} copy(f32[1,1024,1024]{2,1,0:T(8,128)} %subtract_bitcast_fusion) | data formatting | bytes 8388608 | tf_op jit(solution)/shard_map/stack | solution.py:54
  63.2 5.3 %all-to-all-start = ((f32[1,1024,1024]{1,0,2:T(1,128)}), f32[1,1024,1024]{1,0,2:T(1,128)}, u32[]{:S(2)}, u32[]{:S(2)}) async-start(f32[1,1024,1024]{1,0,2:T(1,128)} %copy.13), calls=%async_computation | async-start | bytes 8388608 | tf_op jit(solution)/shard_map/all_to_all | solution.py:60
  69.8 0.8 dynamic-update-slice.3
  70.6 49.3 %all-reduce = s32[8]{0:T(128)S(1)} all-reduce(s32[8]{0:T(128)S(1)} %dynamic-update-slice.3), channel_id=1, replica_groups=mesh['wide'=8,'narrow'=4] {'wide'}, use_global_device_ids=true, to_apply=%add | all-reduce | flops 8 | bytes 64
  119.9 5.2 %copy.17 = f32[1,1024,1024]{1,2,0:T(8,128)} copy(f32[1,1024,1024]{1,0,2:T(1,128)} %all-to-all-done) | data formatting | bytes 8388608
  125.0 5.4 %copy.16 = f32[1,1024,8,128]{3,2,1,0:T(8,128)} copy(f32[1,1024,8,128]{1,3,2,0:T(8,128)} %bitcast.68) | data formatting | bytes 8388608 | tf_op jit(solution)/shard_map/all_to_all | solution.py:60
  130.4 5.6 %fusion = f32[4,1024,128]{2,0,1:T(4,128)} fusion(f32[1,1024,8,128]{3,2,1,0:T(8,128)} %copy.16, s32[8]{0:T(128)S(1)} %all-reduce), kind=kOutput, calls=%fused_computation | convolution fusion | flops 50331680 | bytes 6291488 | tf_op jit(solution)/shard_map/bw,bij->wij/dot_general | solution.py:26
  138.3 1.3 fusion.5
  139.7 42.9 %psum.7 = f32[4,1024]{1,0:T(4,128)S(1)} all-reduce(f32[4,1024]{1,0:T(4,128)S(1)} %broadcast_multiply_fusion), channel_id=1, replica_groups=mesh['wide'=8,'narrow'=4] {'wide','narrow'}, use_global_device_ids=true, to_apply=%region_3.4 | all-reduce | flops 4096 | bytes 32768 | tf_op jit(solution)/shard_map/psum | solution.py:57
  183.1 40.4 %all-reduce.4.cloned.1.call-done = f32[4,1024,128]{2,0,1:T(4,128)} async-done(((f32[4,1024,128]{2,0,1:T(4,128)}), f32[4,1024,128]{2,0,1:T(4,128)}) %all-reduce.4.cloned.1.call-update) | async-done | bytes 2097168
  223.5 1.1 constant_dynamic-slice_fusion
  224.6 0.8 copy.15
  (22 shorter events, 3.1 us)
Async XLA Ops:
  7.2 26.1 %copy-start = (f32[1,512]{1,0:T(1,128)S(1)}, f32[1,512]{1,0:T(1,128)}, u32[]{:S(2)}) copy-start(f32[1,512]{1,0:T(1,128)} %param.8) | copy-start | bytes 6148
  39.8 3.7 %copy-start.1 = (f32[1,512,1024]{2,1,0:T(8,128)S(1)}, f32[1,512,1024]{2,1,0:T(8,128)}, u32[]{:S(2)}) copy-start(f32[1,512,1024]{2,1,0:T(8,128)} %param.7) | copy-start | bytes 6291460
  63.2 6.0 %copy-start.3 = (u32[32]{0:T(128)S(1)}, u32[32]{0:T(128)}, u32[]{:S(2)}) copy-start(u32[32]{0:T(128)} %constant.68) | copy-start | bytes 388
  63.2 56.7 %all-to-all-start = ((f32[1,1024,1024]{1,0,2:T(1,128)}), f32[1,1024,1024]{1,0,2:T(1,128)}, u32[]{:S(2)}, u32[]{:S(2)}) async-start(f32[1,1024,1024]{1,0,2:T(1,128)} %copy.13), calls=%async_computation | async-start | bytes 8388608 | tf_op jit(solution)/shard_map/all_to_all | solution.py:60
  68.5 155.0 %all-reduce.4.cloned.1.call-start = ((), (), s32[]{:S(2)}) async-start(), calls=%async_computation.1 | async-start | bytes 4194304
  136.0 0.7 copy-start.2
Sparse Core Ops, SparseCore 0:
  136.1 87.3 all-reduce.3
where the time goes:
time: 233 us; the launch traced here: 232 us
  blocking collectives  92.2 us (40%)
  waiting for transfers between devices  40.4 us (17%)
  matrix products  27.9 us (12%)
  local copies, waits for them, and re-layouts  26.7 us (11%)
  other arithmetic  23.6 us (10%)
  between operations  16.1 us (7%)
  starting transfers between devices  5.37 us (2%)
    unnamed x1, blocking collectives  49.3 us
    psum x1, blocking collectives, on_device(): rhs_whole = lax.psum(rhs_local, ('wide', 'narrow'))  42.9 us
    unnamed x2, waiting for transfers between devices  40.4 us
    dot_general x7, matrix products, tdot(): lax.dot_general(left, right, (((0,), (0,)), ((), ())), precision=lax.Prec...  20.5 us
    another operation x3, other arithmetic, on_device(): factor = jnp.linalg.cholesky(curv)  12.4 us
    another operation x1, local copies, waits for them, and re-layouts, on_device(): stacked = jnp.stack(schurs, axis=0)  11 us
    another operation x2, other arithmetic, on_device(): jax.scipy.linalg.cho_solve((factor, True), jnp.concatenate([coupling, lr]...  10.5 us
    unnamed x15, local copies, waits for them, and re-layouts  9.63 us
  transfers between devices with their start and end apart: 2, of which 1 were waited for; matrix products, arithmetic and copies ran while one was open for 2% of the time, Pallas kernels for 0%

commit v1 on v0

--- a/solution.py
+++ b/solution.py
@@ -1,3 +1,4 @@
+import functools
 import jax
 import jax.numpy as jnp
 from jax import lax
@@ -5,6 +6,13 @@
 
 WINDOW_PARAMS = 1024
 NWIN = 4
+
+
+def report_skins_all(tile_in, peer_axis):
+    return jax.lax.all_gather(tile_in, peer_axis).sum(axis=0)
+
+
+show_samples_now = functools.partial(report_skins_all, peer_axis=("wide", "narrow"))
 
 
 def tdot(left, right):
@@ -54,7 +62,7 @@
     stacked = jnp.stack(schurs, axis=0)
     rhs_stack = jnp.stack(reduced, axis=0)
     rhs_local = window_sum(windows, rhs_stack[:, :, None])[:, :, 0]
-    rhs_whole = lax.psum(rhs_local, ("wide", "narrow"))
+    rhs_whole = show_samples_now(rhs_local)
     owned = WINDOW_PARAMS // lax.axis_size("narrow")
     normal_rhs = lax.dynamic_slice_in_dim(rhs_whole, lax.axis_index("narrow") * owned, owned, 1)
     received = lax.all_to_all(stacked, "wide", split_axis=2, concat_axis=0, tiled=True)

time: 233 us -> 241 us (1.034)
  blocking collectives: 92.2 us -> 129 us
  waiting for transfers between devices: 40.4 us -> 11.3 us
    all_gather x0 -> x1, blocking collectives: none -> 79.8 us  [report_skins_all(): return jax.lax.all_gather(tile_in, peer_axis).sum(axis=0)]
    psum x1 -> x0, blocking collectives: 42.9 us -> none  [on_device(): rhs_whole = lax.psum(rhs_local, ('wide', 'narrow'))]
    unnamed x2, waiting for transfers between devices: 40.4 us -> 11.3 us
where the time goes in v1:
time: 241 us; the launch traced here: 240 us
  blocking collectives  129 us (54%)
  matrix products  27.9 us (12%)
  local copies, waits for them, and re-layouts  26.7 us (11%)
  other arithmetic  23.7 us (10%)
  between operations  16.1 us (7%)
  waiting for transfers between devices  11.3 us (5%)
  starting transfers between devices  5.37 us (2%)
    all_gather x1, blocking collectives, report_skins_all(): return jax.lax.all_gather(tile_in, peer_axis).sum(axis=0)  79.8 us
    unnamed x1, blocking collectives  49.3 us
    dot_general x7, matrix products, tdot(): lax.dot_general(left, right, (((0,), (0,)), ((), ())), precision=lax.Prec...  20.5 us
    another operation x3, other arithmetic, on_device(): factor = jnp.linalg.cholesky(curv)  12.4 us
    unnamed x2, waiting for transfers between devices  11.3 us
    another operation x1, local copies, waits for them, and re-layouts, on_device(): stacked = jnp.stack(schurs, axis=0)  11 us
    another operation x2, other arithmetic, on_device(): jax.scipy.linalg.cho_solve((factor, True), jnp.concatenate([coupling, lr]...  10.5 us
    unnamed x15, local copies, waits for them, and re-layouts  9.63 us
  transfers between devices with their start and end apart: 2, of which 1 were waited for; matrix products, arithmetic and copies ran while one was open for 2% of the time, Pallas kernels for 0%

profile of v1, /device:TPU:0, one launch (start us, length us, event | category | flops | bytes accessed | tf_op | source)
XLA Modules:
  0.0 240.2 jit_solution(18207338409751753867)
XLA Ops:
  7.8 0.7 fusion.39
  8.5 1.7 fusion.18
  10.4 11.7 %cholesky.17 = f32[128,128]{1,0:T(8,128)S(1)} custom-call(f32[128,128]{1,0:T(8,128)S(1)} %fusion.34), custom_call_target="Cholesky" | custom-call | tf_op jit(solution)/shard_map/jit(cholesky)/cholesky | solution.py:58
  22.1 0.6 compare_reduce_fusion
  22.8 0.7 fusion.29
  23.4 9.8 %custom-call.10 = f32[1,128,128]{1,2,0:T(8,128)S(1)} custom-call(f32[1,128,128]{2,1,0:T(8,128)S(1)} %fusion.29), custom_call_target="InvertDiagBlocksLowerTriangular" | custom-call | tf_op jit(solution)/shard_map/jit(_cho_solve)/triangular_solve | solution.py:59
  33.3 1.6 convolution_bitcast_fusion
  34.9 3.1 %fusion.2 = f32[128,1024]{1,0:T(8,128)S(1)} fusion(f32[1,512,1024]{2,1,0:T(8,128)} %param.7, f32[1,512,128]{2,1,0:T(8,128)} %param.6, f32[512]{0:T(512)S(1)} %fusion.39), kind=kOutput, calls=%fused_computation.3 | convolution fusion | flops 805371904 | bytes 2885632 | tf_op jit(solution)/shard_map/dot_general | solution.py:19
  38.0 0.7 fusion.12
  38.7 1.1 fusion.30
  39.8 3.7 %fusion.16 = f32[1024,1024]{1,0:T(8,128)S(1)} fusion(f32[128,1024]{1,0:T(8,128)S(1)} %fusion.2, f32[128,1025]{0,1:T(8,128)S(1)} %fusion.30), kind=kOutput, calls=%fused_computation.18 | convolution fusion | flops 1610612736 | bytes 5242880 | tf_op jit(solution)/shard_map/dot_general | solution.py:19
  43.5 8.7 %subtract_bitcast_fusion = f32[1,1024,1024]{2,1,0:T(8,128)} fusion(f32[1024,1024]{1,0:T(8,128)S(1)} %fusion.16, f32[1,512,1024]{2,1,0:T(8,128)S(1)} %copy-done.1, f32[512]{0:T(512)S(1)} %fusion.39), kind=kOutput, calls=%fused_computation.2 | convolution fusion | flops 6444023808 | bytes 10487808 | tf_op jit(solution)/shard_map/dot_general | solution.py:19
  52.2 11.0 %copy.13 = f32[1,1024,1024]{1,0,2:T(1,128)} copy(f32[1,1024,1024]{2,1,0:T(8,128)} %subtract_bitcast_fusion) | data formatting | bytes 8388608 | tf_op jit(solution)/shard_map/stack | solution.py:62
  63.2 5.3 %all-to-all-start = ((f32[1,1024,1024]{1,0,2:T(1,128)}), f32[1,1024,1024]{1,0,2:T(1,128)}, u32[]{:S(2)}, u32[]{:S(2)}) async-start(f32[1,1024,1024]{1,0,2:T(1,128)} %copy.13), calls=%async_computation | async-start | bytes 8388608 | tf_op jit(solution)/shard_map/all_to_all | solution.py:68
  69.8 0.8 dynamic-update-slice.3
  70.6 49.3 %all-reduce = s32[8]{0:T(128)S(1)} all-reduce(s32[8]{0:T(128)S(1)} %dynamic-update-slice.3), channel_id=1, replica_groups=mesh['wide'=8,'narrow'=4] {'wide'}, use_global_device_ids=true, to_apply=%add | all-reduce | flops 8 | bytes 64
  119.9 5.2 %copy.17 = f32[1,1024,1024]{1,2,0:T(8,128)} copy(f32[1,1024,1024]{1,0,2:T(1,128)} %all-to-all-done) | data formatting | bytes 8388608
  125.0 5.4 %copy.16 = f32[1,1024,8,128]{3,2,1,0:T(8,128)} copy(f32[1,1024,8,128]{1,3,2,0:T(8,128)} %bitcast.70) | data formatting | bytes 8388608 | tf_op jit(solution)/shard_map/all_to_all | solution.py:68
  130.4 5.6 %fusion = f32[4,1024,128]{2,0,1:T(4,128)} fusion(f32[1,1024,8,128]{3,2,1,0:T(8,128)} %copy.16, s32[8]{0:T(128)S(1)} %all-reduce), kind=kOutput, calls=%fused_computation | convolution fusion | flops 50331680 | bytes 6291488 | tf_op jit(solution)/shard_map/bw,bij->wij/dot_general | solution.py:34
  138.3 1.3 fusion.5
  139.7 79.8 %all-gather.1 = f32[32,4,1024]{2,1,0:T(4,128)S(1)} all-gather(f32[1,4,1024]{2,1,0:T(4,128)S(1)} %multiply_bitcast_fusion), channel_id=2, replica_groups=mesh['wide'=8,'narrow'=4] {'wide','narrow'}, dimensions={0}, use_global_device_ids=true | all-gather | bytes 540672 | tf_op jit(solution)/shard_map/all_gather | solution.py:12
  220.2 11.3 %all-reduce.4.cloned.1.call-done = f32[4,1024,128]{2,0,1:T(4,128)} async-done(((f32[4,1024,128]{2,0,1:T(4,128)}), f32[4,1024,128]{2,0,1:T(4,128)}) %all-reduce.4.cloned.1.call-update) | async-done | bytes 2097168
  231.5 1.1 constant_dynamic-slice_fusion
  232.6 0.8 copy.15
  (23 shorter events, 3.2 us)
Async XLA Ops:
  7.2 26.1 %copy-start = (f32[1,512]{1,0:T(1,128)S(1)}, f32[1,512]{1,0:T(1,128)}, u32[]{:S(2)}) copy-start(f32[1,512]{1,0:T(1,128)} %param.8) | copy-start | bytes 6148
  39.8 3.7 %copy-start.1 = (f32[1,512,1024]{2,1,0:T(8,128)S(1)}, f32[1,512,1024]{2,1,0:T(8,128)}, u32[]{:S(2)}) copy-start(f32[1,512,1024]{2,1,0:T(8,128)} %param.7) | copy-start | bytes 6291460
  63.2 6.0 %copy-start.3 = (u32[32]{0:T(128)S(1)}, u32[32]{0:T(128)}, u32[]{:S(2)}) copy-start(u32[32]{0:T(128)} %constant.68) | copy-start | bytes 388
  63.2 56.7 %all-to-all-start = ((f32[1,1024,1024]{1,0,2:T(1,128)}), f32[1,1024,1024]{1,0,2:T(1,128)}, u32[]{:S(2)}, u32[]{:S(2)}) async-start(f32[1,1024,1024]{1,0,2:T(1,128)} %copy.13), calls=%async_computation | async-start | bytes 8388608 | tf_op jit(solution)/shard_map/all_to_all | solution.py:68
  68.5 163.0 %all-reduce.4.cloned.1.call-start = ((), (), s32[]{:S(2)}) async-start(), calls=%async_computation.1 | async-start | bytes 4194304
  136.0 0.7 copy-start.2
Sparse Core Ops, SparseCore 0:
  136.1 95.3 all-reduce.3
